TPU v7x, 256 devices: a whole 4x4x8 slice. The times are simulated.
256 devices in a mesh: unit: 4 (over y_lo, core), zero: 32 (over z, y_hi, x_hi), cols: 2 (over x_lo).
Axes of the slice: x: 4 (x_hi: 2, x_lo: 2; x = x_hi * 2 + x_lo), y: 4 (y_hi: 2, y_lo: 2; y = y_hi * 2 + y_lo), z: 8, core: 2. Of those that a mesh axis runs over, the one named last changes fastest.
Arguments:
- weight_gate: bfloat16 [20480, 13824], P(('unit', 'zero'), 'cols'), parts along dimension 0, may hold values from -0.15625 to 0.15625
- low_gate: bfloat16 [20480, 32], P(('unit', 'zero')), parts along dimension 0, may hold values from -0.078125 to 0.078125
- high_gate: bfloat16 [128, 13824], P('unit', 'cols'), parts along dimension 0, may hold values from -1 to 1
- weight_up: bfloat16 [20480, 13824], P(('unit', 'zero'), 'cols'), parts along dimension 0, may hold values from -0.15625 to 0.15625
- low_up: bfloat16 [20480, 32], P(('unit', 'zero')), parts along dimension 0, may hold values from -0.078125 to 0.078125
- high_up: bfloat16 [128, 13824], P('unit', 'cols'), parts along dimension 0, may hold values from -1 to 1
- norm_train: float32 [20480], P(('unit', 'zero', 'cols')), parts along dimension 0, may hold values from 0.25 to 1.75
- norm_step: float32 [20480], P(('unit', 'zero', 'cols')), parts along dimension 0, may hold values from -0.3 to 0.3
Outputs:
- final_gate: bfloat16 [20480, 13824], P('unit', ('cols', 'zero')), parts along dimension 0
- final_up: bfloat16 [20480, 13824], P('unit', ('cols', 'zero')), parts along dimension 0
- scale_gate: float32 [55296], P(('unit', 'cols', 'zero')), parts along dimension 0
- scale_up: float32 [55296], P(('unit', 'cols', 'zero')), parts along dimension 0
- serve_norm: bfloat16 [20480], P('unit'), parts along dimension 0
There are 4 independent parts, one for each index of `unit`. A program takes and returns all parts, laid end to end along the dimension named above; each array names one. Nothing has to cross between parts.
All inputs are finite; a program needn't handle non-finite values. Where the computation divides by a largest or mean magnitude, that divisor is 1e-20 or more.
Results may differ from a plain program's by a relative error of at most 0.001.
Values may be sent and summed in bfloat16 or wider, within the bound.
No kernel may reach another device: no remote copies, remote signals or barrier semaphores. Data moves between devices by JAX's collectives and lax.ppermute only.
A program may use at most 128 MiB of HBM per device.

v0:
```python
import jax
import jax.numpy as jnp
from jax import lax
from jax.sharding import PartitionSpec as P

D_MODEL = 5120
mix_rate = 0.5


def copy_for_each(value, axis):
    copies = jnp.broadcast_to(value, (lax.axis_size(axis), *value.shape))
    return lax.all_to_all(copies, axis, split_axis=0, concat_axis=0, tiled=True)


def over_copies(value, axis):
    return copy_for_each(value, axis).sum(axis=0)


def together(arrays, axis):
    vector, at, outs = (jnp.concatenate([a.reshape(-1) for a in arrays]), 0, [])
    total = over_copies(vector, axis)
    for a in arrays:
        outs.append(total[at : at + a.size].reshape(a.shape))
        at += a.size
    return tuple(outs)


def laid_out(blocks, dim):
    blocks = jnp.moveaxis(blocks, 0, dim)
    dims = blocks.shape
    return blocks.reshape(*dims[:dim], dims[dim] * dims[dim + 1], *dims[dim + 2 :])


def gathered_copies(value, axis, dim):
    return laid_out(copy_for_each(value, axis), dim)


def local(weight_gate, low_gate, high_gate, weight_up, low_up, high_up, norm_train, norm_step):
    result_gate = weight_gate.astype(jnp.float32) + mix_rate * jnp.dot(
        low_gate, high_gate, preferred_element_type=jnp.float32
    )
    result_up = weight_up.astype(jnp.float32) + mix_rate * jnp.dot(
        low_up, high_up, preferred_element_type=jnp.float32
    )
    total_gate, total_up = together(
        (jnp.sum(jnp.abs(result_gate), axis=0), jnp.sum(jnp.abs(result_up), axis=0)), "zero"
    )
    scale_gate = total_gate / D_MODEL
    scale_up = total_up / D_MODEL
    narrow_gate, narrow_up = (
        (result_gate / scale_gate).astype(jnp.bfloat16),
        (result_up / scale_up).astype(jnp.bfloat16),
    )
    final_gate, final_up = (
        lax.all_to_all(narrow_gate, "zero", split_axis=1, concat_axis=0, tiled=True),
        lax.all_to_all(narrow_up, "zero", split_axis=1, concat_axis=0, tiled=True),
    )
    place = lax.axis_index("zero")
    scale_gate = lax.dynamic_slice_in_dim(
        scale_gate, place * final_gate.shape[1], final_gate.shape[1]
    )
    scale_up = lax.dynamic_slice_in_dim(scale_up, place * final_up.shape[1], final_up.shape[1])
    serve_norm = gathered_copies((norm_train + norm_step).astype(jnp.bfloat16), ("zero", "cols"), 0)
    return (final_gate, final_up, scale_gate, scale_up, serve_norm)


def solution(mesh):
    in_specs = (
        P(("unit", "zero"), "cols"),
        P(("unit", "zero"), None),
        P("unit", "cols"),
        P(("unit", "zero"), "cols"),
        P(("unit", "zero"), None),
        P("unit", "cols"),
        P(("unit", "zero", "cols")),
        P(("unit", "zero", "cols")),
    )
    out_specs = (
        P("unit", ("cols", "zero")),
        P("unit", ("cols", "zero")),
        P(("unit", "cols", "zero")),
        P(("unit", "cols", "zero")),
        P("unit"),
    )
    return jax.shard_map(local, mesh=mesh, in_specs=in_specs, out_specs=out_specs, check_vma=False)
```

profile of v0, /device:TPU:64, one launch (start us, length us, event | category | flops | bytes accessed | tf_op | source)
XLA Modules:
  0.0 244.0 jit_solution(5626973775937074867)
XLA Ops:
  0.6 0.0 copy-start
  0.6 0.0 copy-start.2
  0.7 0.0 copy-start.1
  0.7 0.0 copy-start.3
  0.7 1.0 copy-done
  1.7 4.7 %abs_reduce_fusion = (f32[6912]{0:T(1024)S(1)}, f32[160,6912]{1,0:T(8,128)}) fusion(bf16[160,32]{0,1:T(8,128)(2,1)} %param.12, bf16[32,6912]{1,0:T(8,128)(2,1)S(1)} %copy-done, bf16[160,6912]{1,0:T(8,128)(2,1)} %param.11), kind=kOutput, calls=%fused_computation.6 | convolution fusion | flops 76301568 | bytes 7115776 | tf_op jit(solution)/shard_map/dot_general | solution.py:42
  6.3 0.0 copy-done.2
  6.3 0.0 copy-done.1
  6.3 0.0 copy-done.3
  6.3 3.1 %abs_reduce_fusion.1 = (f32[6912]{0:T(1024)S(1)}, f32[160,6912]{1,0:T(8,128)}) fusion(bf16[160,32]{0,1:T(8,128)(2,1)S(1)} %copy-done.3, bf16[32,6912]{1,0:T(8,128)(2,1)S(1)} %copy-done.2, bf16[160,6912]{1,0:T(8,128)(2,1)S(1)} %copy-done.1), kind=kOutput, calls=%fused_computation.7 | convolution fusion | flops 76301568 | bytes 7115776 | tf_op jit(solution)/shard_map/dot_general | solution.py:39
  9.4 0.0 copy-start.4
  9.4 0.0 copy-start.5
  9.4 2.1 broadcast_in_dim.8
  11.6 13.4 %all-to-all-start = ((f32[32,1,13824]{2,1,0:T(1,128)}), f32[32,1,13824]{2,1,0:T(1,128)S(1)}, u32[]{:S(2)}, u32[]{:S(2)}) async-start(f32[32,1,13824]{2,1,0:T(1,128)} %broadcast_in_dim.8), calls=%async_computation | async-start | bytes 3538944 | tf_op jit(solution)/shard_map/all_to_all | solution.py:12
  24.9 0.0 copy-done.4
  24.9 0.0 copy-done.5
  25.0 45.9 %all-to-all-done = f32[32,1,13824]{2,1,0:T(1,128)S(1)} async-done(((f32[32,1,13824]{2,1,0:T(1,128)}), f32[32,1,13824]{2,1,0:T(1,128)S(1)}, u32[]{:S(2)}, u32[]{:S(2)}) %all-to-all-start) | async-done | bytes 1769504 | tf_op jit(solution)/shard_map/all_to_all | solution.py:12
  70.9 0.6 broadcast_in_dim.9
  71.5 5.4 %all-to-all-start.3 = ((bf16[64,1,80]{2,1,0:T(2,128)(2,1)}), bf16[64,1,80]{2,1,0:T(2,128)(2,1)S(1)}, u32[]{:S(2)}, u32[]{:S(2)}) async-start(bf16[64,1,80]{2,1,0:T(2,128)(2,1)} %broadcast_in_dim.9), calls=%async_computation.3 | async-start | bytes 65536 | tf_op jit(solution)/shard_map/all_to_all | solution.py:12
  76.9 1.0 reduce_sum.29
  77.9 6.2 %divide_convert_fusion = (bf16[160,6912]{1,0:T(8,128)(2,1)}, bf16[160,6912]{1,0:T(8,128)(2,1)}) fusion(f32[160,6912]{1,0:T(8,128)} %get-tuple-element.28, f32[6912]{0:T(1024)S(1)} %get-tuple-element.25, f32[160,6912]{1,0:T(8,128)} %get-tuple-element.30, f32[6912]{0:T(1024)S(1)} %get-tuple-element.26), kind=kLoop, calls=%fused_computation.4 | loop fusion | flops 4423680 | bytes 13326336 | tf_op jit(solution)/shard_map/convert_element_type | solution.py:52
  84.1 9.0 %all_to_all.37 = bf16[160,32,216]{2,1,0:T(8,128)(2,1)S(1)} reshape(bf16[160,6912]{1,0:T(8,128)(2,1)} %get-tuple-element.32) | data formatting | bytes 4423680 | tf_op jit(solution)/shard_map/all_to_all | solution.py:55
  93.2 3.0 %copy.28 = bf16[160,32,216]{2,0,1:T(8,128)(2,1)} copy(bf16[160,32,216]{2,1,0:T(8,128)(2,1)S(1)} %all_to_all.37) | data formatting | bytes 4423680 | tf_op jit(solution)/shard_map/all_to_all | solution.py:55
  96.2 0.0 all-to-all-done.3
  96.2 12.3 %all-to-all-start.1 = ((bf16[160,32,216]{2,0,1:T(8,128)(2,1)}), bf16[160,32,216]{2,0,1:T(8,128)(2,1)S(1)}, u32[]{:S(2)}, u32[]{:S(2)}) async-start(bf16[160,32,216]{2,0,1:T(8,128)(2,1)} %copy.28), calls=%async_computation.1 | async-start | bytes 5242880 | tf_op jit(solution)/shard_map/all_to_all | solution.py:55
  108.5 9.9 %all_to_all.41 = bf16[160,32,216]{2,1,0:T(8,128)(2,1)} reshape(bf16[160,6912]{1,0:T(8,128)(2,1)} %get-tuple-element.31) | data formatting | bytes 4423680 | tf_op jit(solution)/shard_map/all_to_all | solution.py:56
  118.4 4.7 %copy.29 = bf16[160,32,216]{2,0,1:T(8,128)(2,1)} copy(bf16[160,32,216]{2,1,0:T(8,128)(2,1)} %all_to_all.41) | data formatting | bytes 4423680 | tf_op jit(solution)/shard_map/all_to_all | solution.py:56
  123.1 48.5 %all-to-all-done.1 = bf16[160,32,216]{2,0,1:T(8,128)(2,1)S(1)} async-done(((bf16[160,32,216]{2,0,1:T(8,128)(2,1)}), bf16[160,32,216]{2,0,1:T(8,128)(2,1)S(1)}, u32[]{:S(2)}, u32[]{:S(2)}) %all-to-all-start.1) | async-done | bytes 2211872 | tf_op jit(solution)/shard_map/all_to_all | solution.py:55
  171.6 4.9 %all-to-all-start.2 = ((bf16[160,32,216]{2,0,1:T(8,128)(2,1)}), bf16[160,32,216]{2,0,1:T(8,128)(2,1)}, u32[]{:S(2)}, u32[]{:S(2)}) async-start(bf16[160,32,216]{2,0,1:T(8,128)(2,1)} %copy.29), calls=%async_computation.2 | async-start | bytes 5242880 | tf_op jit(solution)/shard_map/all_to_all | solution.py:56
  176.5 0.1 reduce.1
  176.6 0.7 reshape.30
  177.3 0.6 dynamic_slice.6
  178.0 0.6 dynamic_slice.7
  178.6 2.5 %copy.30 = bf16[5120,216]{0,1:T(8,128)(2,1)} copy(bf16[5120,216]{1,0:T(8,128)(2,1)S(1)} %bitcast.10) | data formatting | bytes 4423680
  181.1 58.6 %all-to-all-done.2 = bf16[160,32,216]{2,0,1:T(8,128)(2,1)} async-done(((bf16[160,32,216]{2,0,1:T(8,128)(2,1)}), bf16[160,32,216]{2,0,1:T(8,128)(2,1)}, u32[]{:S(2)}, u32[]{:S(2)}) %all-to-all-start.2) | async-done | bytes 2211872 | tf_op jit(solution)/shard_map/all_to_all | solution.py:56
  239.7 4.3 %copy.31 = bf16[5120,216]{0,1:T(8,128)(2,1)} copy(bf16[5120,216]{1,0:T(8,128)(2,1)} %bitcast.3) | data formatting | bytes 4423680
  (3 shorter events, 0.0 us)
Async XLA Ops:
  0.6 1.0 copy-start
  0.6 5.7 %copy-start.2 = (bf16[32,6912]{1,0:T(8,128)(2,1)S(1)}, bf16[32,6912]{1,0:T(8,128)(2,1)}, u32[]{:S(2)}) copy-start(bf16[32,6912]{1,0:T(8,128)(2,1)} %param.10) | copy-start | bytes 1327108
  0.7 5.7 %copy-start.1 = (bf16[160,6912]{1,0:T(8,128)(2,1)S(1)}, bf16[160,6912]{1,0:T(8,128)(2,1)}, u32[]{:S(2)}) copy-start(bf16[160,6912]{1,0:T(8,128)(2,1)} %param.8) | copy-start | bytes 6635524
  0.7 5.7 %copy-start.3 = (bf16[160,32]{0,1:T(8,128)(2,1)S(1)}, bf16[160,32]{0,1:T(8,128)(2,1)}, u32[]{:S(2)}) copy-start(bf16[160,32]{0,1:T(8,128)(2,1)} %param.9) | copy-start | bytes 30724
  9.4 15.5 %copy-start.4 = (f32[80]{0:T(128)S(1)}, f32[80]{0:T(128)}, u32[]{:S(2)}) copy-start(f32[80]{0:T(128)} %param.14) | copy-start | bytes 964
  9.4 15.5 %copy-start.5 = (f32[80]{0:T(128)S(1)}, f32[80]{0:T(128)}, u32[]{:S(2)}) copy-start(f32[80]{0:T(128)} %param.15) | copy-start | bytes 964
  11.6 59.3 %all-to-all-start = ((f32[32,1,13824]{2,1,0:T(1,128)}), f32[32,1,13824]{2,1,0:T(1,128)S(1)}, u32[]{:S(2)}, u32[]{:S(2)}) async-start(f32[32,1,13824]{2,1,0:T(1,128)} %broadcast_in_dim.8), calls=%async_computation | async-start | bytes 3538944 | tf_op jit(solution)/shard_map/all_to_all | solution.py:12
  71.5 24.7 %all-to-all-start.3 = ((bf16[64,1,80]{2,1,0:T(2,128)(2,1)}), bf16[64,1,80]{2,1,0:T(2,128)(2,1)S(1)}, u32[]{:S(2)}, u32[]{:S(2)}) async-start(bf16[64,1,80]{2,1,0:T(2,128)(2,1)} %broadcast_in_dim.9), calls=%async_computation.3 | async-start | bytes 65536 | tf_op jit(solution)/shard_map/all_to_all | solution.py:12
  96.2 75.4 %all-to-all-start.1 = ((bf16[160,32,216]{2,0,1:T(8,128)(2,1)}), bf16[160,32,216]{2,0,1:T(8,128)(2,1)S(1)}, u32[]{:S(2)}, u32[]{:S(2)}) async-start(bf16[160,32,216]{2,0,1:T(8,128)(2,1)} %copy.28), calls=%async_computation.1 | async-start | bytes 5242880 | tf_op jit(solution)/shard_map/all_to_all | solution.py:55
  171.6 68.1 %all-to-all-start.2 = ((bf16[160,32,216]{2,0,1:T(8,128)(2,1)}), bf16[160,32,216]{2,0,1:T(8,128)(2,1)}, u32[]{:S(2)}, u32[]{:S(2)}) async-start(bf16[160,32,216]{2,0,1:T(8,128)(2,1)} %copy.29), calls=%async_computation.2 | async-start | bytes 5242880 | tf_op jit(solution)/shard_map/all_to_all | solution.py:56
where the time goes:
time: 245 us; the launch traced here: 244 us
  waiting for transfers between devices  153 us (62%)
  local copies, waits for them, and re-layouts  39.1 us (16%)
  starting transfers between devices  35.9 us (15%)
  matrix products  7.76 us (3%)
  other arithmetic  7.35 us (3%)
    all_to_all x1, waiting for transfers between devices, local(): lax.all_to_all(narrow_up, 'zero', split_axis=1, concat_axis=0, tiled=True)  58.6 us
    all_to_all x1, waiting for transfers between devices, local(): lax.all_to_all(narrow_gate, 'zero', split_axis=1, concat_axis=0, tiled=True)  48.5 us
    all_to_all x2, waiting for transfers between devices, copy_for_each(): return lax.all_to_all(copies, axis, split_axis=0, concat_axis=0, tiled=True)  45.9 us
    all_to_all x2, starting transfers between devices, copy_for_each(): return lax.all_to_all(copies, axis, split_axis=0, concat_axis=0, tiled=True)  18.7 us
    all_to_all x2, local copies, waits for them, and re-layouts, local(): lax.all_to_all(narrow_up, 'zero', split_axis=1, concat_axis=0, tiled=True)  14.6 us
    all_to_all x1, starting transfers between devices, local(): lax.all_to_all(narrow_gate, 'zero', split_axis=1, concat_axis=0, tiled=True)  12.3 us
    all_to_all x2, local copies, waits for them, and re-layouts, local(): lax.all_to_all(narrow_gate, 'zero', split_axis=1, concat_axis=0, tiled=True)  12 us
    unnamed x14, local copies, waits for them, and re-layouts  7.74 us
  transfers between devices with their start and end apart: 4, of which 3 were waited for; matrix products, arithmetic and copies ran while one was open for 8% of the time, Pallas kernels for 0%

commit v1 on v0

--- a/solution.py
+++ b/solution.py
@@ -52,7 +52,12 @@
         (result_up / scale_up).astype(jnp.bfloat16),
     )
     final_gate, final_up = (
-        lax.all_to_all(narrow_gate, "zero", split_axis=1, concat_axis=0, tiled=True),
+        jnp.concatenate(
+            lax.all_to_all(
+                jnp.stack(jnp.split(narrow_gate, lax.axis_size("zero"), axis=1)), "zero", 0, 0
+            ),
+            axis=0,
+        ),
         lax.all_to_all(narrow_up, "zero", split_axis=1, concat_axis=0, tiled=True),
     )
     place = lax.axis_index("zero")

time: 245 us -> 233 us (0.951)
  local copies, waits for them, and re-layouts: 39.1 us -> 31.4 us
    all_to_all x2 -> x0, local copies, waits for them, and re-layouts: 12 us -> none  [local(): lax.all_to_all(narrow_gate, 'zero', split_axis=1, concat_axis=0, tiled=True)]
    unnamed x14 -> x47, local copies, waits for them, and re-layouts: 7.74 us -> 11.9 us
    all_to_all x1, waiting for transfers between devices: 48.5 us -> 44.6 us  [local(): lax.all_to_all(jnp.stack(jnp.split(narrow_gate, lax.axis_size('zero'), ax...]
    convert_element_type x0 -> x1, other arithmetic: none -> 2.53 us  [local(): (result_gate / scale_gate).astype(jnp.bfloat16)]
  transfers between devices with their start and end apart: 4 -> 4, of which waited for: 3 -> 4; matrix products, arithmetic and copies ran while one was open for 8% -> 8% of each run, Pallas kernels for 0% -> 0%
where the time goes in v1:
time: 233 us
  waiting for transfers between devices  151 us (65%)
  starting transfers between devices  33.9 us (15%)
  local copies, waits for them, and re-layouts  31.4 us (13%)
  matrix products  7.79 us (3%)
  other arithmetic  7.53 us (3%)
    all_to_all x1, waiting for transfers between devices, local(): lax.all_to_all(narrow_up, 'zero', split_axis=1, concat_axis=0, tiled=True)  58.6 us
    all_to_all x2, waiting for transfers between devices, copy_for_each(): return lax.all_to_all(copies, axis, split_axis=0, concat_axis=0, tiled=True)  47.9 us
    all_to_all x1, waiting for transfers between devices, local(): lax.all_to_all(jnp.stack(jnp.split(narrow_gate, lax.axis_size('zero'), ax...  44.6 us
    all_to_all x2, starting transfers between devices, copy_for_each(): return lax.all_to_all(copies, axis, split_axis=0, concat_axis=0, tiled=True)  18.7 us
    all_to_all x2, local copies, waits for them, and re-layouts, local(): lax.all_to_all(narrow_up, 'zero', split_axis=1, concat_axis=0, tiled=True)  14.6 us
    unnamed x47, local copies, waits for them, and re-layouts  11.9 us
    all_to_all x1, starting transfers between devices, local(): lax.all_to_all(jnp.stack(jnp.split(narrow_gate, lax.axis_size('zero'), ax...  10.3 us
    all_to_all x1, starting transfers between devices, local(): lax.all_to_all(narrow_up, 'zero', split_axis=1, concat_axis=0, tiled=True)  4.89 us
  transfers between devices with their start and end apart: 4, of which 4 were waited for; matrix products, arithmetic and copies ran while one was open for 8% of the time, Pallas kernels for 0%

profile of v1, /device:TPU:64, one launch (start us, length us, event | category | flops | bytes accessed | tf_op | source)
XLA Modules:
  0.0 232.8 jit_solution(81916017146663212)
XLA Ops:
  0.7 1.0 copy-done
  1.7 4.7 %abs_reduce_fusion.1 = (f32[6912]{0:T(1024)S(1)}, f32[160,6912]{1,0:T(8,128)}) fusion(bf16[160,32]{0,1:T(8,128)(2,1)} %param.9, bf16[32,6912]{1,0:T(8,128)(2,1)S(1)} %copy-done, bf16[160,6912]{1,0:T(8,128)(2,1)} %param.8), kind=kOutput, calls=%fused_computation.7 | convolution fusion | flops 76301568 | bytes 7115776 | tf_op jit(solution)/shard_map/dot_general | solution.py:39
  6.4 3.1 %abs_reduce_fusion = (f32[6912]{0:T(1024)S(1)}, f32[160,6912]{1,0:T(8,128)}) fusion(bf16[160,32]{0,1:T(8,128)(2,1)S(1)} %copy-done.4, bf16[32,6912]{1,0:T(8,128)(2,1)S(1)} %copy-done.3, bf16[160,6912]{1,0:T(8,128)(2,1)S(1)} %copy-done.2), kind=kOutput, calls=%fused_computation.6 | convolution fusion | flops 76301568 | bytes 7115776 | tf_op jit(solution)/shard_map/dot_general | solution.py:42
  9.5 2.1 broadcast_in_dim.8
  11.6 13.4 %all-to-all-start = ((f32[32,1,13824]{2,1,0:T(1,128)}), f32[32,1,13824]{2,1,0:T(1,128)S(1)}, u32[]{:S(2)}, u32[]{:S(2)}) async-start(f32[32,1,13824]{2,1,0:T(1,128)} %broadcast_in_dim.8), calls=%async_computation | async-start | bytes 3538944 | tf_op jit(solution)/shard_map/all_to_all | solution.py:12
  25.0 45.9 %all-to-all-done = f32[32,1,13824]{2,1,0:T(1,128)S(1)} async-done(((f32[32,1,13824]{2,1,0:T(1,128)}), f32[32,1,13824]{2,1,0:T(1,128)S(1)}, u32[]{:S(2)}, u32[]{:S(2)}) %all-to-all-start) | async-done | bytes 1769504 | tf_op jit(solution)/shard_map/all_to_all | solution.py:12
  70.9 0.6 broadcast_in_dim.9
  71.6 5.4 %all-to-all-start.3 = ((bf16[64,1,80]{2,1,0:T(2,128)(2,1)}), bf16[64,1,80]{2,1,0:T(2,128)(2,1)S(1)}, u32[]{:S(2)}, u32[]{:S(2)}) async-start(bf16[64,1,80]{2,1,0:T(2,128)(2,1)} %broadcast_in_dim.9), calls=%async_computation.3 | async-start | bytes 65536 | tf_op jit(solution)/shard_map/all_to_all | solution.py:12
  76.9 1.0 reduce_sum.29
  78.0 2.5 %divide_convert_fusion.1 = bf16[160,6912]{1,0:T(8,128)(2,1)S(1)} fusion(f32[160,6912]{1,0:T(8,128)} %get-tuple-element.35, f32[6912]{0:T(1024)S(1)} %get-tuple-element.31), kind=kLoop, calls=%fused_computation.5 | loop fusion | flops 2211840 | bytes 6663168 | tf_op jit(solution)/shard_map/convert_element_type | solution.py:51
  80.5 0.1 fusion.32
  80.6 0.1 fusion.31
  80.7 0.1 fusion.30
  80.8 0.1 fusion.29
  80.9 0.1 fusion.28
  81.0 0.1 fusion.27
  81.1 0.1 fusion.26
  81.2 0.1 fusion.25
  81.3 0.1 fusion.24
  81.4 0.1 fusion.23
  81.6 0.1 fusion.21
  81.7 0.1 fusion.20
  81.9 0.1 fusion.18
  82.0 0.1 fusion.16
  82.1 0.1 fusion.15
  82.3 0.1 fusion.13
  82.4 0.1 fusion.12
  82.6 0.1 fusion.10
  82.7 0.1 fusion.9
  82.9 0.1 fusion.7
  83.1 0.1 fusion.5
  83.2 0.1 fusion.4
  83.4 0.1 fusion.2
  83.5 1.5 copy-done.1
  85.0 2.0 all-to-all-done.3
  87.0 10.3 %all-to-all-start.1 = ((bf16[32,160,216]{2,1,0:T(8,128)(2,1)}), bf16[32,160,216]{2,1,0:T(8,128)(2,1)S(1)}, u32[]{:S(2)}, u32[]{:S(2)}) async-start(bf16[32,160,216]{2,1,0:T(8,128)(2,1)} %copy-done.1), calls=%async_computation.1 | async-start | bytes 5242880 | tf_op jit(solution)/shard_map/all_to_all | solution.py:56
  97.3 3.9 %divide_convert_fusion = bf16[160,6912]{1,0:T(8,128)(2,1)} fusion(f32[160,6912]{1,0:T(8,128)} %get-tuple-element.33, f32[6912]{0:T(1024)S(1)} %get-tuple-element.30), kind=kLoop, calls=%fused_computation.4 | loop fusion | flops 2211840 | bytes 6663168 | tf_op jit(solution)/shard_map/convert_element_type | solution.py:52
  101.2 9.9 %all_to_all.27 = bf16[160,32,216]{2,1,0:T(8,128)(2,1)} reshape(bf16[160,6912]{1,0:T(8,128)(2,1)} %divide_convert_fusion) | data formatting | bytes 4423680 | tf_op jit(solution)/shard_map/all_to_all | solution.py:61
  111.1 4.7 %copy.25 = bf16[160,32,216]{2,0,1:T(8,128)(2,1)} copy(bf16[160,32,216]{2,1,0:T(8,128)(2,1)} %all_to_all.27) | data formatting | bytes 4423680 | tf_op jit(solution)/shard_map/all_to_all | solution.py:61
  115.8 44.6 %all-to-all-done.1 = bf16[32,160,216]{2,1,0:T(8,128)(2,1)S(1)} async-done(((bf16[32,160,216]{2,1,0:T(8,128)(2,1)}), bf16[32,160,216]{2,1,0:T(8,128)(2,1)S(1)}, u32[]{:S(2)}, u32[]{:S(2)}) %all-to-all-start.1) | async-done | bytes 2211872 | tf_op jit(solution)/shard_map/all_to_all | solution.py:56
  160.5 4.9 %all-to-all-start.2 = ((bf16[160,32,216]{2,0,1:T(8,128)(2,1)}), bf16[160,32,216]{2,0,1:T(8,128)(2,1)}, u32[]{:S(2)}, u32[]{:S(2)}) async-start(bf16[160,32,216]{2,0,1:T(8,128)(2,1)} %copy.25), calls=%async_computation.2 | async-start | bytes 5242880 | tf_op jit(solution)/shard_map/all_to_all | solution.py:61
  165.4 0.1 reduce.1
  165.5 0.7 reshape.31
  166.2 0.6 dynamic_slice.6
  166.8 0.6 dynamic_slice.7
  167.4 2.5 %copy.26 = bf16[5120,216]{0,1:T(8,128)(2,1)} copy(bf16[5120,216]{1,0:T(8,128)(2,1)S(1)} %bitcast.136) | data formatting | bytes 4423680
  169.9 58.6 %all-to-all-done.2 = bf16[160,32,216]{2,0,1:T(8,128)(2,1)} async-done(((bf16[160,32,216]{2,0,1:T(8,128)(2,1)}), bf16[160,32,216]{2,0,1:T(8,128)(2,1)}, u32[]{:S(2)}, u32[]{:S(2)}) %all-to-all-start.2) | async-done | bytes 2211872 | tf_op jit(solution)/shard_map/all_to_all | solution.py:61
  228.5 4.3 %copy.27 = bf16[5120,216]{0,1:T(8,128)(2,1)} copy(bf16[5120,216]{1,0:T(8,128)(2,1)} %bitcast.34) | data formatting | bytes 4423680
  (24 shorter events, 0.7 us)
Async XLA Ops:
  0.6 1.0 copy-start
  0.6 5.7 %copy-start.4 = (bf16[160,32]{0,1:T(8,128)(2,1)S(1)}, bf16[160,32]{0,1:T(8,128)(2,1)}, u32[]{:S(2)}) copy-start(bf16[160,32]{0,1:T(8,128)(2,1)} %param.12) | copy-start | bytes 30724
  0.7 5.7 %copy-start.3 = (bf16[32,6912]{1,0:T(8,128)(2,1)S(1)}, bf16[32,6912]{1,0:T(8,128)(2,1)}, u32[]{:S(2)}) copy-start(bf16[32,6912]{1,0:T(8,128)(2,1)} %param.13) | copy-start | bytes 1327108
  0.7 5.7 %copy-start.2 = (bf16[160,6912]{1,0:T(8,128)(2,1)S(1)}, bf16[160,6912]{1,0:T(8,128)(2,1)}, u32[]{:S(2)}) copy-start(bf16[160,6912]{1,0:T(8,128)(2,1)} %param.11) | copy-start | bytes 6635524
  9.5 15.5 %copy-start.5 = (f32[80]{0:T(128)S(1)}, f32[80]{0:T(128)}, u32[]{:S(2)}) copy-start(f32[80]{0:T(128)} %param.14) | copy-start | bytes 964
  9.5 15.5 %copy-start.6 = (f32[80]{0:T(128)S(1)}, f32[80]{0:T(128)}, u32[]{:S(2)}) copy-start(f32[80]{0:T(128)} %param.15) | copy-start | bytes 964
  11.6 59.3 %all-to-all-start = ((f32[32,1,13824]{2,1,0:T(1,128)}), f32[32,1,13824]{2,1,0:T(1,128)S(1)}, u32[]{:S(2)}, u32[]{:S(2)}) async-start(f32[32,1,13824]{2,1,0:T(1,128)} %broadcast_in_dim.8), calls=%async_computation | async-start | bytes 3538944 | tf_op jit(solution)/shard_map/all_to_all | solution.py:12
  71.6 15.4 %all-to-all-start.3 = ((bf16[64,1,80]{2,1,0:T(2,128)(2,1)}), bf16[64,1,80]{2,1,0:T(2,128)(2,1)S(1)}, u32[]{:S(2)}, u32[]{:S(2)}) async-start(bf16[64,1,80]{2,1,0:T(2,128)(2,1)} %broadcast_in_dim.9), calls=%async_computation.3 | async-start | bytes 65536 | tf_op jit(solution)/shard_map/all_to_all | solution.py:12
  83.5 1.5 copy-start.1
  87.0 73.4 %all-to-all-start.1 = ((bf16[32,160,216]{2,1,0:T(8,128)(2,1)}), bf16[32,160,216]{2,1,0:T(8,128)(2,1)S(1)}, u32[]{:S(2)}, u32[]{:S(2)}) async-start(bf16[32,160,216]{2,1,0:T(8,128)(2,1)} %copy-done.1), calls=%async_computation.1 | async-start | bytes 5242880 | tf_op jit(solution)/shard_map/all_to_all | solution.py:56
  160.5 68.1 %all-to-all-start.2 = ((bf16[160,32,216]{2,0,1:T(8,128)(2,1)}), bf16[160,32,216]{2,0,1:T(8,128)(2,1)}, u32[]{:S(2)}, u32[]{:S(2)}) async-start(bf16[160,32,216]{2,0,1:T(8,128)(2,1)} %copy.25), calls=%async_computation.2 | async-start | bytes 5242880 | tf_op jit(solution)/shard_map/all_to_all | solution.py:61
